TPU v7x, 32 devices: a whole 2x2x4 slice. The times are simulated.
32 devices in a mesh: curve: 8 (over z, x), head: 4 (over y, core).
Axes of the slice: x: 2, y: 2, z: 4, core: 2. Of those that a mesh axis runs over, the one named last changes fastest.
Arguments:
- points: bfloat16 [16384, 1024], P(('curve', 'head')), may hold values from -6 to 6
- order: int32 [32, 512], P(('curve', 'head')), may hold values from 0 to 511, each once within a row
- scan_ids: int32 [16384], P(('curve', 'head')), may hold values from 0 to 3
- ln_gain: float32 [2, 1024], replicated, may hold values from 0.25 to 1.75
- w_qkv: bfloat16 [2, 1024, 3072], P(None, None, 'head'), may hold values from -7 to 7, as said below
- w_out: bfloat16 [2, 1024, 1024], P(None, 'head'), may hold values from -0.1875 to 0.1875
Outputs:
- refined: bfloat16 [16384, 1024], P(('curve', 'head'))
Inputs may be any that keep to these rules, and one draw needn't show every extreme that they name: `order`: row b is a permutation of the 512 rows of block b. `w_qkv`: columns ordered by head, then query, key, value, then entry.
All inputs are finite; a program needn't handle non-finite values.
Results may differ from a plain program's by a relative error of at most 0.01.
Values may be sent and summed in bfloat16 or wider, within the bound.
A program may use at most 64 MiB of HBM per device.

v0:
```python
import jax
import jax.numpy as jnp
from jax import lax
from jax.sharding import PartitionSpec as P

HEAD_DIM = 64
PATCH = 1024
EPSILON = 1e-05


def extended(array, sides, width):
    for axis, dim in sides:
        peers, length = (lax.axis_size(axis), array.shape[dim])
        up = [(i, (i + 1) % peers) for i in range(peers)]
        down = [(j, i) for i, j in up]
        last = lax.slice_in_dim(array, length - width, length, axis=dim)
        first = lax.slice_in_dim(array, 0, width, axis=dim)
        before = lax.ppermute(last, axis, up)
        after = lax.ppermute(first, axis, down)
        array = jnp.concatenate([before, array, after], axis=dim)
    return array


def layer_norm(rows, gain):
    values = rows.astype(jnp.float32)
    center = values - jnp.mean(values, axis=-1, keepdims=True)
    spread = jnp.mean(center * center, axis=-1, keepdims=True)
    return (center * lax.rsqrt(spread + EPSILON) * gain).astype(jnp.bfloat16)


def plain_window(first_row):
    return first_row // PATCH * PATCH


def centred_window(first_row):
    return (first_row + PATCH // 2) // PATCH * PATCH


def attend(queries, keys, values, query_tags, key_tags, window_of):
    block_rows = PATCH // 2
    blocks_count = queries.shape[0] // block_rows

    def one_block(block_index):
        first_row = block_index * block_rows
        query_block = lax.dynamic_slice_in_dim(queries, first_row, block_rows, 0)
        tags_block = lax.dynamic_slice_in_dim(query_tags, first_row, block_rows, 0)
        first_key = window_of(first_row)
        key_block = lax.dynamic_slice_in_dim(keys, first_key, PATCH, 0)
        value_block = lax.dynamic_slice_in_dim(values, first_key, PATCH, 0)
        key_block_tags = lax.dynamic_slice_in_dim(key_tags, first_key, PATCH, 0)
        scores = jnp.einsum(
            "qhd,khd->hqk", query_block, key_block, preferred_element_type=jnp.float32
        ) * HEAD_DIM ** (-0.5)
        allowed = tags_block[:, None] == key_block_tags[None, :]
        scores = jnp.where(allowed[None], scores, -jnp.inf)
        row_max = jnp.max(scores, axis=-1, keepdims=True)
        expo = jnp.exp(scores - row_max)
        probs = (expo / jnp.sum(expo, axis=-1, keepdims=True)).astype(jnp.bfloat16)
        result = jnp.einsum("hqk,khd->qhd", probs, value_block, preferred_element_type=jnp.float32)
        return result.astype(jnp.bfloat16)

    outputs = lax.map(one_block, jnp.arange(blocks_count))
    return outputs.reshape(queries.shape[0], -1)


def on_device(points, order, scan_ids, ln_gain, w_qkv, w_out):
    stream = points[order[0]]
    range_ids = lax.all_gather(scan_ids, "head", axis=0, tiled=True)
    span_rows = range_ids.shape[0]
    heads_local = w_qkv.shape[2] // (3 * HEAD_DIM)
    half_patch = PATCH // 2
    for layer_index in range(2):
        normed = layer_norm(stream, ln_gain[layer_index])
        weights_here = w_qkv[layer_index]
        qkv_span = jnp.dot(
            lax.all_gather(normed, "head", axis=0, tiled=True),
            weights_here,
            preferred_element_type=jnp.float32,
        ).astype(jnp.bfloat16)
        pieces = qkv_span.reshape(span_rows, heads_local, 3, HEAD_DIM)
        if layer_index == 0:
            attended = attend(
                pieces[:, :, 0],
                pieces[:, :, 1],
                pieces[:, :, 2],
                range_ids,
                range_ids,
                plain_window,
            )
        else:
            tags_float = range_ids.astype(jnp.bfloat16)
            kv_flat = pieces[:, :, 1:].reshape(span_rows, heads_local * 2 * HEAD_DIM)
            wide_kv, wide_tags = (
                extended(kv_flat, (("curve", 0),), half_patch),
                extended(tags_float, (("curve", 0),), half_patch),
            )
            wide_pieces = wide_kv.reshape(-1, heads_local, 2, HEAD_DIM)
            attended = attend(
                pieces[:, :, 0],
                wide_pieces[:, :, 0],
                wide_pieces[:, :, 1],
                range_ids,
                wide_tags.astype(jnp.int32),
                centred_window,
            )
        heads_rows = lax.all_to_all(attended, "head", split_axis=0, concat_axis=1, tiled=True)
        update = jnp.dot(
            heads_rows,
            lax.all_gather(w_out[layer_index], "head", axis=0, tiled=True),
            preferred_element_type=jnp.float32,
        )
        stream = (stream.astype(jnp.float32) + update).astype(jnp.bfloat16)
    return stream


def solution(mesh):
    in_specs = (
        P(("curve", "head"), None),
        P(("curve", "head"), None),
        P(("curve", "head")),
        P(),
        P(None, None, "head"),
        P(None, "head", None),
    )
    out_specs = P(("curve", "head"), None)
    return jax.shard_map(
        on_device, mesh=mesh, in_specs=in_specs, out_specs=out_specs, check_vma=False
    )
```

profile of v0, /device:TPU:0, one launch (start us, length us, event | category | flops | bytes accessed | tf_op | source)
XLA Modules:
  0.0 295.6 jit_solution(13849537120225569016)
XLA Ops:
  6.5 0.8 compare_select_fusion
  7.3 0.5 copy-done
  7.8 2.0 gather_fusion
  10.1 0.4 fusion.67
  10.5 1.3 fusion.69
  12.0 1.1 fusion.103
  13.1 6.2 %all-gather.2 = s32[4,1,512]{2,1,0:T(1,128)S(1)} all-gather(s32[1,1,512]{2,1,0:T(1,128)S(1)} %bitcast.103), channel_id=1, replica_groups=mesh['curve'=8,'head'=4] {'head'}, dimensions={0}, use_global_device_ids=true | all-gather | bytes 10240 | tf_op jit(solution)/shard_map/all_gather | solution.py:68
  19.3 29.9 %all-gather.8.cloned.1.call-done = bf16[2048,1024]{1,0:T(8,128)(2,1)} async-done(((bf16[512,1024]{1,0:T(8,128)(2,1)}), bf16[2048,1024]{1,0:T(8,128)(2,1)}) %all-gather.8.cloned.1.call-update) | async-done | bytes 4194320 | tf_op jit(solution)/shard_map/all_gather | solution.py:76
  49.2 6.1 %convolution_convert_fusion.1 = bf16[2048,768]{0,1:T(8,128)(2,1)S(1)} fusion(bf16[2048,1024]{1,0:T(8,128)(2,1)} %all-gather.8.cloned.1.call-done, bf16[2,1024,768]{2,1,0:T(8,128)(2,1)} %param.14), kind=kOutput, calls=%fused_computation.52 | convolution fusion | flops 3222798336 | bytes 8912896 | tf_op jit(solution)/shard_map/dot_general | solution.py:75
  55.4 1.7 slice_bitcast_fusion.3
  57.0 1.1 broadcast.125.clone
  58.1 58.1 %while.24 = (s32[]{:T(128)}, bf16[4,512,4,64]{1,3,2,0:T(8,128)(2,1)}, s32[4]{0:T(128)S(1)}, bf16[2048,4,64]{0,2,1:T(8,128)(2,1)}, s32[2048]{0:T(1024)S(1)}, /*in...) while((s32[]{:T(128)}, ...), condition=%wide.region_5.6_spmd, body=%wide.region_2.5_spmd.sunk | while | flops 550110208 | bytes 19434388 | solution.py:62
  58.1 0.6 dynamic_slice.136
  59.5 0.4 broadcast_compare_fusion.4
  59.9 7.0 %fusion.123 = (f32[4,512]{1,0:T(4,128)S(1)}, f32[4,512,1024]{2,1,0:T(8,128)}) fusion(pred[512,1024]{1,0:T(8,128)(4,1)S(1)} %broadcast_compare_fusion.4, bf16[2048,4,64]{0,2,1:T(8,128)(2,1)S(1)} %get-tuple-element.384, s32[]{:T(128)S(6)} %select_n.99, bf16[2048,4,64]{0,2,1:T(8,128)(2,1)} %get-tuple-element.383, s32[]{:T(128)S(6)} %select_n.100), kind=kOutput, calls=%fused_computation.93.clone.1 | convolution fusion | flops 276825088 | bytes 9707528 | tf_op jit(solution)/shard_map/while/body/eval_jaxpr/sub | solution.py:57
  66.9 5.8 %fusion.124 = bf16[4,512,4,64]{1,3,2,0:T(8,128)(2,1)} fusion(bf16[4,512,4,64]{1,3,2,0:T(8,128)(2,1)} %get-tuple-element.364, s32[]{:T(128)} %get-tuple-element.363, f32[4,512,1024]{2,1,0:T(8,128)} %get-tuple-element.336, f32[4,512]{1,0:T(4,128)S(1)} %get-tuple-element.337, bf16[2048,4,64]{0,2,1:T(8,128)(2,1)} %get-tuple-element.381, s32[]{:T(128)S(6)} %select_n.99), kind=kOutput, calls=%fused_computation.12.clone.1 | convolution fusion | flops 272760832 | bytes 9183748 | tf_op jit(solution)/shard_map/while/body/eval_jaxpr/hqk,khd->qhd/dot_general | solution.py:59
  72.7 0.6 dynamic_slice.136
  74.0 0.4 broadcast_compare_fusion.4
  74.4 7.0 %fusion.123 = (f32[4,512]{1,0:T(4,128)S(1)}, f32[4,512,1024]{2,1,0:T(8,128)}) fusion(pred[512,1024]{1,0:T(8,128)(4,1)S(1)} %broadcast_compare_fusion.4, bf16[2048,4,64]{0,2,1:T(8,128)(2,1)S(1)} %get-tuple-element.384, s32[]{:T(128)S(6)} %select_n.99, bf16[2048,4,64]{0,2,1:T(8,128)(2,1)} %get-tuple-element.383, s32[]{:T(128)S(6)} %select_n.100), kind=kOutput, calls=%fused_computation.93.clone.1 | convolution fusion | flops 276825088 | bytes 9707528 | tf_op jit(solution)/shard_map/while/body/eval_jaxpr/sub | solution.py:57
  81.4 5.7 %fusion.124 = bf16[4,512,4,64]{1,3,2,0:T(8,128)(2,1)} fusion(bf16[4,512,4,64]{1,3,2,0:T(8,128)(2,1)} %get-tuple-element.364, s32[]{:T(128)} %get-tuple-element.363, f32[4,512,1024]{2,1,0:T(8,128)} %get-tuple-element.336, f32[4,512]{1,0:T(4,128)S(1)} %get-tuple-element.337, bf16[2048,4,64]{0,2,1:T(8,128)(2,1)} %get-tuple-element.381, s32[]{:T(128)S(6)} %select_n.99), kind=kOutput, calls=%fused_computation.12.clone.1 | convolution fusion | flops 272760832 | bytes 9183748 | tf_op jit(solution)/shard_map/while/body/eval_jaxpr/hqk,khd->qhd/dot_general | solution.py:59
  87.2 0.6 dynamic_slice.136
  88.6 0.4 broadcast_compare_fusion.4
  88.9 7.0 %fusion.123 = (f32[4,512]{1,0:T(4,128)S(1)}, f32[4,512,1024]{2,1,0:T(8,128)}) fusion(pred[512,1024]{1,0:T(8,128)(4,1)S(1)} %broadcast_compare_fusion.4, bf16[2048,4,64]{0,2,1:T(8,128)(2,1)S(1)} %get-tuple-element.384, s32[]{:T(128)S(6)} %select_n.99, bf16[2048,4,64]{0,2,1:T(8,128)(2,1)} %get-tuple-element.383, s32[]{:T(128)S(6)} %select_n.100), kind=kOutput, calls=%fused_computation.93.clone.1 | convolution fusion | flops 276825088 | bytes 9707528 | tf_op jit(solution)/shard_map/while/body/eval_jaxpr/sub | solution.py:57
  95.9 5.7 %fusion.124 = bf16[4,512,4,64]{1,3,2,0:T(8,128)(2,1)} fusion(bf16[4,512,4,64]{1,3,2,0:T(8,128)(2,1)} %get-tuple-element.364, s32[]{:T(128)} %get-tuple-element.363, f32[4,512,1024]{2,1,0:T(8,128)} %get-tuple-element.336, f32[4,512]{1,0:T(4,128)S(1)} %get-tuple-element.337, bf16[2048,4,64]{0,2,1:T(8,128)(2,1)} %get-tuple-element.381, s32[]{:T(128)S(6)} %select_n.99), kind=kOutput, calls=%fused_computation.12.clone.1 | convolution fusion | flops 272760832 | bytes 9183748 | tf_op jit(solution)/shard_map/while/body/eval_jaxpr/hqk,khd->qhd/dot_general | solution.py:59
  101.7 0.6 dynamic_slice.136
  103.1 0.4 broadcast_compare_fusion.4
  103.4 7.0 %fusion.123 = (f32[4,512]{1,0:T(4,128)S(1)}, f32[4,512,1024]{2,1,0:T(8,128)}) fusion(pred[512,1024]{1,0:T(8,128)(4,1)S(1)} %broadcast_compare_fusion.4, bf16[2048,4,64]{0,2,1:T(8,128)(2,1)S(1)} %get-tuple-element.384, s32[]{:T(128)S(6)} %select_n.99, bf16[2048,4,64]{0,2,1:T(8,128)(2,1)} %get-tuple-element.383, s32[]{:T(128)S(6)} %select_n.100), kind=kOutput, calls=%fused_computation.93.clone.1 | convolution fusion | flops 276825088 | bytes 9707528 | tf_op jit(solution)/shard_map/while/body/eval_jaxpr/sub | solution.py:57
  110.5 5.7 %fusion.124 = bf16[4,512,4,64]{1,3,2,0:T(8,128)(2,1)} fusion(bf16[4,512,4,64]{1,3,2,0:T(8,128)(2,1)} %get-tuple-element.364, s32[]{:T(128)} %get-tuple-element.363, f32[4,512,1024]{2,1,0:T(8,128)} %get-tuple-element.336, f32[4,512]{1,0:T(4,128)S(1)} %get-tuple-element.337, bf16[2048,4,64]{0,2,1:T(8,128)(2,1)} %get-tuple-element.381, s32[]{:T(128)S(6)} %select_n.99), kind=kOutput, calls=%fused_computation.12.clone.1 | convolution fusion | flops 272760832 | bytes 9183748 | tf_op jit(solution)/shard_map/while/body/eval_jaxpr/hqk,khd->qhd/dot_general | solution.py:59
  116.2 3.5 %all-to-all-start = ((bf16[4,512,256]{1,2,0:T(8,128)(2,1)}), bf16[4,512,256]{1,2,0:T(8,128)(2,1)S(1)}, u32[]{:S(2)}, u32[]{:S(2)}) async-start(bf16[4,512,256]{1,2,0:T(8,128)(2,1)} %bitcast.16), calls=%async_computation | async-start | bytes 2097152 | tf_op jit(solution)/shard_map/all_to_all | solution.py:106
  120.0 14.1 %all-to-all-done = bf16[4,512,256]{1,2,0:T(8,128)(2,1)S(1)} async-done(((bf16[4,512,256]{1,2,0:T(8,128)(2,1)}), bf16[4,512,256]{1,2,0:T(8,128)(2,1)S(1)}, u32[]{:S(2)}, u32[]{:S(2)}) %all-to-all-start) | async-done | bytes 1048608 | tf_op jit(solution)/shard_map/all_to_all | solution.py:106
  134.1 2.9 convert_reduce_fusion
  137.1 0.4 fusion.64
  137.5 1.4 fusion.66
  139.0 1.5 collective-permute-start.2
  140.5 3.3 %collective-permute-start.3 = (bf16[512]{0:T(512)(128)(2,1)S(1)}, bf16[512]{0:T(512)(128)(2,1)S(1)}, u32[]{:S(2)}, u32[]{:S(2)}) collective-permute-start(bf16[512]{0:T(512)(128)(2,1)S(1)} %get-tuple-element.245), channel_id=1, source_target_pairs={{4,0},{8,4},{12,8},{16,12},{20,16},{24,20},{28,24},{0,28},{5,1},{9... | collective-permute-start | bytes 3080 | tf_op jit(solution)/shard_map/ppermute | solution.py:19
  143.8 29.7 %all-gather.10.cloned.1.call-done = bf16[2048,1024]{1,0:T(8,128)(2,1)} async-done(((bf16[512,1024]{1,0:T(8,128)(2,1)}), bf16[2048,1024]{1,0:T(8,128)(2,1)}) %all-gather.10.cloned.1.call-update) | async-done | bytes 4194320 | tf_op jit(solution)/shard_map/all_gather | solution.py:76
  173.5 6.1 %convolution_convert_fusion = bf16[2048,768]{0,1:T(8,128)(2,1)S(1)} fusion(bf16[2048,1024]{1,0:T(8,128)(2,1)} %all-gather.10.cloned.1.call-done, bf16[2,1024,768]{2,1,0:T(8,128)(2,1)} %param.14), kind=kOutput, calls=%fused_computation.51 | convolution fusion | flops 3222798336 | bytes 8912896 | tf_op jit(solution)/shard_map/dot_general | solution.py:75
  179.7 1.5 collective-permute-start
  181.3 3.3 %collective-permute-start.1 = (bf16[512,512]{0,1:T(8,128)(2,1)S(1)}, bf16[512,512]{0,1:T(8,128)(2,1)S(1)}, u32[]{:S(2)}, u32[]{:S(2)}) collective-permute-start(bf16[512,512]{0,1:T(8,128)(2,1)S(1)} %bitcast.97), channel_id=1, source_target_pairs={{4,0},{8,4},{12,8},{16,12},{20,16},{24,20},{28,24},{0,28},{5,1},{9... | collective-permute-start | bytes 1572872 | tf_op jit(solution)/shard_map/ppermute | solution.py:19
  184.8 1.1 slice_bitcast_fusion.2
  185.9 18.2 %collective-permute-done = bf16[512,512]{0,1:T(8,128)(2,1)S(1)} collective-permute-done((bf16[512,512]{0,1:T(8,128)(2,1)S(1)}, bf16[512,512]{0,1:T(8,128)(2,1)S(1)}, u32[]{:S(2)}, u32[]{:S(2)}) %collective-permute-start) | collective-permute-done | bytes 524320 | tf_op jit(solution)/shard_map/ppermute | solution.py:18
  204.1 2.2 collective-permute-done.1
  206.6 1.4 slice_bitcast_fusion
  208.1 1.1 broadcast.125
  209.1 58.0 %while.25 = (s32[]{:T(128)}, bf16[4,512,4,64]{1,3,2,0:T(8,128)(2,1)}, s32[4]{0:T(128)S(1)}, bf16[3072,4,64]{0,2,1:T(8,128)(2,1)}, s32[2048]{0:T(1024)S(1)}, /*in...) while((s32[]{:T(128)}, ...), condition=%wide.region_11.12_spmd, body=%wide.region_8.11_spmd.sunk | while | flops 550110208 | bytes 19434436 | solution.py:62
  209.1 0.6 dynamic_slice.142
  210.5 0.4 broadcast_compare_fusion.5
  210.9 7.0 %fusion.128 = (f32[4,512]{1,0:T(4,128)S(1)}, f32[4,512,1024]{2,1,0:T(8,128)}) fusion(pred[512,1024]{1,0:T(8,128)(4,1)S(1)} %broadcast_compare_fusion.5, bf16[3072,4,64]{0,2,1:T(8,128)(2,1)S(1)} %get-tuple-element.436, s32[]{:T(128)S(6)} %select_n.103, bf16[2048,4,64]{0,2,1:T(8,128)(2,1)} %get-tuple-element.435, s32[]{:T(128)S(6)} %select_n.104), kind=kOutput, calls=%fused_computation.94.clone.1 | convolution fusion | flops 276825088 | bytes 9707528 | tf_op jit(solution)/shard_map/while/body/eval_jaxpr/sub | solution.py:57
  217.9 5.7 %fusion.129 = bf16[4,512,4,64]{1,3,2,0:T(8,128)(2,1)} fusion(bf16[4,512,4,64]{1,3,2,0:T(8,128)(2,1)} %get-tuple-element.412, s32[]{:T(128)} %get-tuple-element.411, f32[4,512,1024]{2,1,0:T(8,128)} %get-tuple-element.346, f32[4,512]{1,0:T(4,128)S(1)} %get-tuple-element.347, bf16[3072,4,64]{0,2,1:T(8,128)(2,1)} %get-tuple-element.432, s32[]{:T(128)S(6)} %select_n.103), kind=kOutput, calls=%fused_computation.37.clone.1 | convolution fusion | flops 272760832 | bytes 9183748 | tf_op jit(solution)/shard_map/while/body/eval_jaxpr/hqk,khd->qhd/dot_general | solution.py:59
  223.6 0.6 dynamic_slice.142
  225.0 0.4 broadcast_compare_fusion.5
  225.4 7.0 %fusion.128 = (f32[4,512]{1,0:T(4,128)S(1)}, f32[4,512,1024]{2,1,0:T(8,128)}) fusion(pred[512,1024]{1,0:T(8,128)(4,1)S(1)} %broadcast_compare_fusion.5, bf16[3072,4,64]{0,2,1:T(8,128)(2,1)S(1)} %get-tuple-element.436, s32[]{:T(128)S(6)} %select_n.103, bf16[2048,4,64]{0,2,1:T(8,128)(2,1)} %get-tuple-element.435, s32[]{:T(128)S(6)} %select_n.104), kind=kOutput, calls=%fused_computation.94.clone.1 | convolution fusion | flops 276825088 | bytes 9707528 | tf_op jit(solution)/shard_map/while/body/eval_jaxpr/sub | solution.py:57
  232.4 5.7 %fusion.129 = bf16[4,512,4,64]{1,3,2,0:T(8,128)(2,1)} fusion(bf16[4,512,4,64]{1,3,2,0:T(8,128)(2,1)} %get-tuple-element.412, s32[]{:T(128)} %get-tuple-element.411, f32[4,512,1024]{2,1,0:T(8,128)} %get-tuple-element.346, f32[4,512]{1,0:T(4,128)S(1)} %get-tuple-element.347, bf16[3072,4,64]{0,2,1:T(8,128)(2,1)} %get-tuple-element.432, s32[]{:T(128)S(6)} %select_n.103), kind=kOutput, calls=%fused_computation.37.clone.1 | convolution fusion | flops 272760832 | bytes 9183748 | tf_op jit(solution)/shard_map/while/body/eval_jaxpr/hqk,khd->qhd/dot_general | solution.py:59
  238.2 0.6 dynamic_slice.142
  239.5 0.4 broadcast_compare_fusion.5
  239.9 7.0 %fusion.128 = (f32[4,512]{1,0:T(4,128)S(1)}, f32[4,512,1024]{2,1,0:T(8,128)}) fusion(pred[512,1024]{1,0:T(8,128)(4,1)S(1)} %broadcast_compare_fusion.5, bf16[3072,4,64]{0,2,1:T(8,128)(2,1)S(1)} %get-tuple-element.436, s32[]{:T(128)S(6)} %select_n.103, bf16[2048,4,64]{0,2,1:T(8,128)(2,1)} %get-tuple-element.435, s32[]{:T(128)S(6)} %select_n.104), kind=kOutput, calls=%fused_computation.94.clone.1 | convolution fusion | flops 276825088 | bytes 9707528 | tf_op jit(solution)/shard_map/while/body/eval_jaxpr/sub | solution.py:57
  246.9 5.7 %fusion.129 = bf16[4,512,4,64]{1,3,2,0:T(8,128)(2,1)} fusion(bf16[4,512,4,64]{1,3,2,0:T(8,128)(2,1)} %get-tuple-element.412, s32[]{:T(128)} %get-tuple-element.411, f32[4,512,1024]{2,1,0:T(8,128)} %get-tuple-element.346, f32[4,512]{1,0:T(4,128)S(1)} %get-tuple-element.347, bf16[3072,4,64]{0,2,1:T(8,128)(2,1)} %get-tuple-element.432, s32[]{:T(128)S(6)} %select_n.103), kind=kOutput, calls=%fused_computation.37.clone.1 | convolution fusion | flops 272760832 | bytes 9183748 | tf_op jit(solution)/shard_map/while/body/eval_jaxpr/hqk,khd->qhd/dot_general | solution.py:59
  252.7 0.6 dynamic_slice.142
  254.0 0.4 broadcast_compare_fusion.5
  254.4 7.0 %fusion.128 = (f32[4,512]{1,0:T(4,128)S(1)}, f32[4,512,1024]{2,1,0:T(8,128)}) fusion(pred[512,1024]{1,0:T(8,128)(4,1)S(1)} %broadcast_compare_fusion.5, bf16[3072,4,64]{0,2,1:T(8,128)(2,1)S(1)} %get-tuple-element.436, s32[]{:T(128)S(6)} %select_n.103, bf16[2048,4,64]{0,2,1:T(8,128)(2,1)} %get-tuple-element.435, s32[]{:T(128)S(6)} %select_n.104), kind=kOutput, calls=%fused_computation.94.clone.1 | convolution fusion | flops 276825088 | bytes 9707528 | tf_op jit(solution)/shard_map/while/body/eval_jaxpr/sub | solution.py:57
  261.4 5.7 %fusion.129 = bf16[4,512,4,64]{1,3,2,0:T(8,128)(2,1)} fusion(bf16[4,512,4,64]{1,3,2,0:T(8,128)(2,1)} %get-tuple-element.412, s32[]{:T(128)} %get-tuple-element.411, f32[4,512,1024]{2,1,0:T(8,128)} %get-tuple-element.346, f32[4,512]{1,0:T(4,128)S(1)} %get-tuple-element.347, bf16[3072,4,64]{0,2,1:T(8,128)(2,1)} %get-tuple-element.432, s32[]{:T(128)S(6)} %select_n.103), kind=kOutput, calls=%fused_computation.37.clone.1 | convolution fusion | flops 272760832 | bytes 9183748 | tf_op jit(solution)/shard_map/while/body/eval_jaxpr/hqk,khd->qhd/dot_general | solution.py:59
  267.2 3.5 %all-to-all-start.1 = ((bf16[4,512,256]{1,2,0:T(8,128)(2,1)}), bf16[4,512,256]{1,2,0:T(8,128)(2,1)S(1)}, u32[]{:S(2)}, u32[]{:S(2)}) async-start(bf16[4,512,256]{1,2,0:T(8,128)(2,1)} %bitcast.30), calls=%async_computation.1 | async-start | bytes 2097152 | tf_op jit(solution)/shard_map/all_to_all | solution.py:106
  270.7 14.4 %all-to-all-done.1 = bf16[4,512,256]{1,2,0:T(8,128)(2,1)S(1)} async-done(((bf16[4,512,256]{1,2,0:T(8,128)(2,1)}), bf16[4,512,256]{1,2,0:T(8,128)(2,1)S(1)}, u32[]{:S(2)}, u32[]{:S(2)}) %all-to-all-start.1) | async-done | bytes 1048608 | tf_op jit(solution)/shard_map/all_to_all | solution.py:106
  285.1 3.9 %fusion.71 = bf16[512,1024]{1,0:T(8,128)(2,1)} fusion(bf16[512,1024]{1,0:T(8,128)(2,1)S(1)} %get-tuple-element.247, bf16[512,1024]{0,1:T(8,128)(2,1)S(1)} %bitcast.94, bf16[1,1024,1024]{2,1,0:T(8,128)(2,1)} %all-gather.14.cloned.1.call-done), kind=kOutput, calls=%fused_computation.71 | convolution fusion | flops 1075314688 | bytes 5242880 | tf_op jit(solution)/shard_map/dot_general | solution.py:107
  (52 shorter events, 2.1 us)
Async XLA Ops:
  6.5 1.2 copy-start
  6.5 42.7 %all-gather.8.cloned.1.call-start = ((), (), s32[]{:S(2)}) async-start(), calls=%async_computation.2 | async-start | bytes 5242880 | tf_op jit(solution)/shard_map/all_gather | solution.py:76
  7.8 2.7 copy-start.3
  9.8 2.1 copy-start.2
  10.5 2.6 copy-start.4
  11.9 108.1 %all-gather.12.cloned.1.call-start = ((), (), s32[]{:S(2)}) async-start(), calls=%async_computation.4 | async-start | bytes 2621440 | tf_op jit(solution)/shard_map/all_gather | solution.py:109
  116.2 17.9 %all-to-all-start = ((bf16[4,512,256]{1,2,0:T(8,128)(2,1)}), bf16[4,512,256]{1,2,0:T(8,128)(2,1)S(1)}, u32[]{:S(2)}, u32[]{:S(2)}) async-start(bf16[4,512,256]{1,2,0:T(8,128)(2,1)} %bitcast.16), calls=%async_computation | async-start | bytes 2097152 | tf_op jit(solution)/shard_map/all_to_all | solution.py:106
  119.7 53.8 %all-gather.10.cloned.1.call-start = ((), (), s32[]{:S(2)}) async-start(), calls=%async_computation.3 | async-start | bytes 5242880 | tf_op jit(solution)/shard_map/all_gather | solution.py:76
  138.9 131.8 %all-gather.14.cloned.1.call-start = ((), (), s32[]{:S(2)}) async-start(), calls=%async_computation.5 | async-start | bytes 2621440 | tf_op jit(solution)/shard_map/all_gather | solution.py:109
  139.0 45.6 %collective-permute-start.2 = (bf16[512]{0:T(512)(128)(2,1)S(1)}, bf16[512]{0:T(512)(128)(2,1)S(1)}, u32[]{:S(2)}, u32[]{:S(2)}) collective-permute-start(bf16[512]{0:T(512)(128)(2,1)S(1)} %get-tuple-element.244), channel_id=1, source_target_pairs={{0,4},{4,8},{8,12},{12,16},{16,20},{20,24},{24,28},{28,0},{1,5},{5... | collective-permute-start | bytes 3080 | tf_op jit(solution)/shard_map/ppermute | solution.py:18
  140.5 44.1 %collective-permute-start.3 = (bf16[512]{0:T(512)(128)(2,1)S(1)}, bf16[512]{0:T(512)(128)(2,1)S(1)}, u32[]{:S(2)}, u32[]{:S(2)}) collective-permute-start(bf16[512]{0:T(512)(128)(2,1)S(1)} %get-tuple-element.245), channel_id=1, source_target_pairs={{4,0},{8,4},{12,8},{16,12},{20,16},{24,20},{28,24},{0,28},{5,1},{9... | collective-permute-start | bytes 3080 | tf_op jit(solution)/shard_map/ppermute | solution.py:19
  179.7 24.3 %collective-permute-start = (bf16[512,512]{0,1:T(8,128)(2,1)S(1)}, bf16[512,512]{0,1:T(8,128)(2,1)S(1)}, u32[]{:S(2)}, u32[]{:S(2)}) collective-permute-start(bf16[512,512]{0,1:T(8,128)(2,1)S(1)} %bitcast.98), channel_id=1, source_target_pairs={{0,4},{4,8},{8,12},{12,16},{16,20},{20,24},{24,28},{28,0},{1,5},{5... | collective-permute-start | bytes 1572872 | tf_op jit(solution)/shard_map/ppermute | solution.py:18
  181.3 25.0 %collective-permute-start.1 = (bf16[512,512]{0,1:T(8,128)(2,1)S(1)}, bf16[512,512]{0,1:T(8,128)(2,1)S(1)}, u32[]{:S(2)}, u32[]{:S(2)}) collective-permute-start(bf16[512,512]{0,1:T(8,128)(2,1)S(1)} %bitcast.97), channel_id=1, source_target_pairs={{4,0},{8,4},{12,8},{16,12},{20,16},{24,20},{28,24},{0,28},{5,1},{9... | collective-permute-start | bytes 1572872 | tf_op jit(solution)/shard_map/ppermute | solution.py:19
  267.2 17.9 %all-to-all-start.1 = ((bf16[4,512,256]{1,2,0:T(8,128)(2,1)}), bf16[4,512,256]{1,2,0:T(8,128)(2,1)S(1)}, u32[]{:S(2)}, u32[]{:S(2)}) async-start(bf16[4,512,256]{1,2,0:T(8,128)(2,1)} %bitcast.30), calls=%async_computation.1 | async-start | bytes 2097152 | tf_op jit(solution)/shard_map/all_to_all | solution.py:106
  285.1 3.9 %copy-start.1 = (bf16[512,1024]{1,0:T(8,128)(2,1)S(1)}, bf16[512,1024]{1,0:T(8,128)(2,1)}, u32[]{:S(2)}) copy-start(bf16[512,1024]{1,0:T(8,128)(2,1)} %param.10) | copy-start | bytes 3145732
Sparse Core Ops, SparseCore 0:
  12.0 37.1 all-gather.7
  50.8 22.5 all-gather.11
  139.0 34.4 all-gather.9
  174.9 22.5 all-gather.13
where the time goes:
time: 296 us
  matrix products  121 us (41%)
  waiting for transfers between devices  109 us (37%)
  starting transfers between devices  16.9 us (6%)
  local copies, waits for them, and re-layouts  15.9 us (5%)
  between operations  13.3 us (4%)
  other arithmetic  7.79 us (3%)
  blocking collectives  6.2 us (2%)
  loops' own time  5.57 us (2%)
    all_gather x2, waiting for transfers between devices, on_device(): lax.all_gather(normed, 'head', axis=0, tiled=True)  59.7 us
    sub x8, matrix products, one_block(): expo = jnp.exp(scores - row_max)  56.2 us
    dot_general x8, matrix products, one_block(): jnp.einsum('hqk,khd->qhd', probs, value_block, preferred_element_type=jnp...  45.9 us
    all_to_all x2, waiting for transfers between devices, on_device(): lax.all_to_all(attended, 'head', split_axis=0, concat_axis=1, tiled=True)  28.5 us
    ppermute x2, waiting for transfers between devices, extended(): before = lax.ppermute(last, axis, up)  18.2 us
    dot_general x2, matrix products, on_device(): jnp.dot(lax.all_gather(normed, 'head', axis=0, tiled=True), weights_here,...  12.3 us
    all_to_all x2, starting transfers between devices, on_device(): lax.all_to_all(attended, 'head', split_axis=0, concat_axis=1, tiled=True)  7.03 us
    dot_general x2, matrix products, on_device(): jnp.dot(heads_rows, lax.all_gather(w_out[layer_index], 'head', axis=0, ti...  6.86 us
  transfers between devices with their start and end apart: 10, of which 6 were waited for; matrix products, arithmetic and copies ran while one was open for 44% of the time, Pallas kernels for 0%

commit v1 on v0

--- a/solution.py
+++ b/solution.py
@@ -6,6 +6,11 @@
 HEAD_DIM = 64
 PATCH = 1024
 EPSILON = 1e-05
+
+
+def all_by_exchange(array, axis, dim):
+    stack = jnp.stack([array] * lax.axis_size(axis))
+    return jnp.concatenate(lax.all_to_all(stack, axis, 0, 0), axis=dim)
 
 
 def extended(array, sides, width):
@@ -73,9 +78,7 @@
         normed = layer_norm(stream, ln_gain[layer_index])
         weights_here = w_qkv[layer_index]
         qkv_span = jnp.dot(
-            lax.all_gather(normed, "head", axis=0, tiled=True),
-            weights_here,
-            preferred_element_type=jnp.float32,
+            all_by_exchange(normed, "head", 0), weights_here, preferred_element_type=jnp.float32
         ).astype(jnp.bfloat16)
         pieces = qkv_span.reshape(span_rows, heads_local, 3, HEAD_DIM)
         if layer_index == 0:

time: 296 us -> 359 us (1.21)
  blocking collectives: 6.2 us -> 59.9 us
  starting transfers between devices: 16.9 us -> 27.9 us
  waiting for transfers between devices: 109 us -> 103 us
  local copies, waits for them, and re-layouts: 15.9 us -> 20.4 us
    all_gather x2 -> x0, waiting for transfers between devices: 59.7 us -> none  [on_device(): lax.all_gather(normed, 'head', axis=0, tiled=True)]
    all_to_all x0 -> x2, waiting for transfers between devices: none -> 53.9 us  [all_by_exchange(): return jnp.concatenate(lax.all_to_all(stack, axis, 0, 0), axis=dim)]
    all_gather x1, blocking collectives: 6.2 us -> 59.9 us  [on_device(): range_ids = lax.all_gather(scan_ids, 'head', axis=0, tiled=True)]
    all_to_all x0 -> x2, starting transfers between devices: none -> 9.82 us  [all_by_exchange(): return jnp.concatenate(lax.all_to_all(stack, axis, 0, 0), axis=dim)]
    another operation x2 -> x4, local copies, waits for them, and re-layouts: 2.15 us -> 7.18 us  [the longest x2 5.04 us: all_by_exchange(): stack = jnp.stack([array] * lax.axis_size(axis))]
  transfers between devices with their start and end apart: 10 -> 10, of which waited for: 6 -> 5; matrix products, arithmetic and copies ran while one was open for 44% -> 37% of each run, Pallas kernels for 0% -> 0%
where the time goes in v1:
time: 359 us; the launch traced here: 358 us
  matrix products  122 us (34%)
  waiting for transfers between devices  103 us (29%)
  blocking collectives  59.9 us (17%)
  starting transfers between devices  27.9 us (8%)
  local copies, waits for them, and re-layouts  20.4 us (6%)
  between operations  13.6 us (4%)
  other arithmetic  5.85 us (2%)
  loops' own time  5.56 us (2%)
    all_gather x1, blocking collectives, on_device(): range_ids = lax.all_gather(scan_ids, 'head', axis=0, tiled=True)  59.9 us
    sub x8, matrix products, one_block(): expo = jnp.exp(scores - row_max)  56.7 us
    all_to_all x2, waiting for transfers between devices, all_by_exchange(): return jnp.concatenate(lax.all_to_all(stack, axis, 0, 0), axis=dim)  53.9 us
    dot_general x8, matrix products, one_block(): jnp.einsum('hqk,khd->qhd', probs, value_block, preferred_element_type=jnp...  45.9 us
    all_to_all x2, waiting for transfers between devices, on_device(): lax.all_to_all(attended, 'head', split_axis=0, concat_axis=1, tiled=True)  28.6 us
    ppermute x2, waiting for transfers between devices, extended(): before = lax.ppermute(last, axis, up)  18.7 us
    dot_general x2, matrix products, on_device(): jnp.dot(all_by_exchange(normed, 'head', 0), weights_here, preferred_eleme...  12.3 us
    all_to_all x2, starting transfers between devices, all_by_exchange(): return jnp.concatenate(lax.all_to_all(stack, axis, 0, 0), axis=dim)  9.82 us
  transfers between devices with their start and end apart: 10, of which 5 were waited for; matrix products, arithmetic and copies ran while one was open for 37% of the time, Pallas kernels for 0%

profile of v1, /device:TPU:0, one launch (start us, length us, event | category | flops | bytes accessed | tf_op | source)
XLA Modules:
  0.0 358.3 jit_solution(17093716993064580837)
XLA Ops:
  6.5 0.8 compare_select_fusion
  7.3 0.5 copy-done
  7.8 2.0 gather_fusion
  10.1 0.4 fusion.67
  10.5 0.4 fusion.69
  10.9 2.5 stack.4
  13.4 5.0 %all-to-all-start = ((bf16[4,512,1024]{2,1,0:T(8,128)(2,1)}), bf16[4,512,1024]{2,1,0:T(8,128)(2,1)}, u32[]{:S(2)}, u32[]{:S(2)}) async-start(bf16[4,512,1024]{2,1,0:T(8,128)(2,1)} %stack.4), calls=%async_computation | async-start | bytes 8388608 | tf_op jit(solution)/shard_map/all_to_all | solution.py:13
  18.5 1.1 fusion.103
  19.6 59.9 %all-gather.2 = s32[4,1,512]{2,1,0:T(1,128)S(1)} all-gather(s32[1,1,512]{2,1,0:T(1,128)S(1)} %bitcast.105), channel_id=1, replica_groups=mesh['curve'=8,'head'=4] {'head'}, dimensions={0}, use_global_device_ids=true | all-gather | bytes 10240 | tf_op jit(solution)/shard_map/all_gather | solution.py:73
  79.4 6.1 %convolution_convert_fusion.1 = bf16[2048,768]{0,1:T(8,128)(2,1)S(1)} fusion(bf16[2048,1024]{1,0:T(8,128)(2,1)} %bitcast.9, bf16[2,1024,768]{2,1,0:T(8,128)(2,1)} %param.14), kind=kOutput, calls=%fused_computation.52 | convolution fusion | flops 3222798336 | bytes 8912896 | tf_op jit(solution)/shard_map/dot_general | solution.py:80
  85.6 1.7 slice_bitcast_fusion.3
  87.2 1.1 broadcast.139.clone
  88.3 58.1 %while.24 = (s32[]{:T(128)}, bf16[4,512,4,64]{1,3,2,0:T(8,128)(2,1)}, s32[4]{0:T(128)S(1)}, bf16[2048,4,64]{0,2,1:T(8,128)(2,1)}, s32[2048]{0:T(1024)S(1)}, /*in...) while((s32[]{:T(128)}, ...), condition=%wide.region_5.6_spmd, body=%wide.region_2.5_spmd.sunk | while | flops 550110208 | bytes 19434388 | solution.py:67
  88.3 0.6 dynamic_slice.136
  89.7 0.4 broadcast_compare_fusion.4
  90.0 7.0 %fusion.123 = (f32[4,512]{1,0:T(4,128)S(1)}, f32[4,512,1024]{2,1,0:T(8,128)}) fusion(pred[512,1024]{1,0:T(8,128)(4,1)S(1)} %broadcast_compare_fusion.4, bf16[2048,4,64]{0,2,1:T(8,128)(2,1)S(1)} %get-tuple-element.384, s32[]{:T(128)S(6)} %select_n.99, bf16[2048,4,64]{0,2,1:T(8,128)(2,1)} %get-tuple-element.383, s32[]{:T(128)S(6)} %select_n.100), kind=kOutput, calls=%fused_computation.93.clone.1 | convolution fusion | flops 276825088 | bytes 9707528 | tf_op jit(solution)/shard_map/while/body/eval_jaxpr/sub | solution.py:62
  97.1 5.7 %fusion.124 = bf16[4,512,4,64]{1,3,2,0:T(8,128)(2,1)} fusion(bf16[4,512,4,64]{1,3,2,0:T(8,128)(2,1)} %get-tuple-element.364, s32[]{:T(128)} %get-tuple-element.363, f32[4,512,1024]{2,1,0:T(8,128)} %get-tuple-element.336, f32[4,512]{1,0:T(4,128)S(1)} %get-tuple-element.337, bf16[2048,4,64]{0,2,1:T(8,128)(2,1)} %get-tuple-element.381, s32[]{:T(128)S(6)} %select_n.99), kind=kOutput, calls=%fused_computation.12.clone.1 | convolution fusion | flops 272760832 | bytes 9183748 | tf_op jit(solution)/shard_map/while/body/eval_jaxpr/hqk,khd->qhd/dot_general | solution.py:64
  102.8 0.6 dynamic_slice.136
  104.2 0.4 broadcast_compare_fusion.4
  104.6 7.0 %fusion.123 = (f32[4,512]{1,0:T(4,128)S(1)}, f32[4,512,1024]{2,1,0:T(8,128)}) fusion(pred[512,1024]{1,0:T(8,128)(4,1)S(1)} %broadcast_compare_fusion.4, bf16[2048,4,64]{0,2,1:T(8,128)(2,1)S(1)} %get-tuple-element.384, s32[]{:T(128)S(6)} %select_n.99, bf16[2048,4,64]{0,2,1:T(8,128)(2,1)} %get-tuple-element.383, s32[]{:T(128)S(6)} %select_n.100), kind=kOutput, calls=%fused_computation.93.clone.1 | convolution fusion | flops 276825088 | bytes 9707528 | tf_op jit(solution)/shard_map/while/body/eval_jaxpr/sub | solution.py:62
  111.6 5.7 %fusion.124 = bf16[4,512,4,64]{1,3,2,0:T(8,128)(2,1)} fusion(bf16[4,512,4,64]{1,3,2,0:T(8,128)(2,1)} %get-tuple-element.364, s32[]{:T(128)} %get-tuple-element.363, f32[4,512,1024]{2,1,0:T(8,128)} %get-tuple-element.336, f32[4,512]{1,0:T(4,128)S(1)} %get-tuple-element.337, bf16[2048,4,64]{0,2,1:T(8,128)(2,1)} %get-tuple-element.381, s32[]{:T(128)S(6)} %select_n.99), kind=kOutput, calls=%fused_computation.12.clone.1 | convolution fusion | flops 272760832 | bytes 9183748 | tf_op jit(solution)/shard_map/while/body/eval_jaxpr/hqk,khd->qhd/dot_general | solution.py:64
  117.3 0.6 dynamic_slice.136
  118.7 0.4 broadcast_compare_fusion.4
  119.1 7.0 %fusion.123 = (f32[4,512]{1,0:T(4,128)S(1)}, f32[4,512,1024]{2,1,0:T(8,128)}) fusion(pred[512,1024]{1,0:T(8,128)(4,1)S(1)} %broadcast_compare_fusion.4, bf16[2048,4,64]{0,2,1:T(8,128)(2,1)S(1)} %get-tuple-element.384, s32[]{:T(128)S(6)} %select_n.99, bf16[2048,4,64]{0,2,1:T(8,128)(2,1)} %get-tuple-element.383, s32[]{:T(128)S(6)} %select_n.100), kind=kOutput, calls=%fused_computation.93.clone.1 | convolution fusion | flops 276825088 | bytes 9707528 | tf_op jit(solution)/shard_map/while/body/eval_jaxpr/sub | solution.py:62
  126.1 5.7 %fusion.124 = bf16[4,512,4,64]{1,3,2,0:T(8,128)(2,1)} fusion(bf16[4,512,4,64]{1,3,2,0:T(8,128)(2,1)} %get-tuple-element.364, s32[]{:T(128)} %get-tuple-element.363, f32[4,512,1024]{2,1,0:T(8,128)} %get-tuple-element.336, f32[4,512]{1,0:T(4,128)S(1)} %get-tuple-element.337, bf16[2048,4,64]{0,2,1:T(8,128)(2,1)} %get-tuple-element.381, s32[]{:T(128)S(6)} %select_n.99), kind=kOutput, calls=%fused_computation.12.clone.1 | convolution fusion | flops 272760832 | bytes 9183748 | tf_op jit(solution)/shard_map/while/body/eval_jaxpr/hqk,khd->qhd/dot_general | solution.py:64
  131.8 0.6 dynamic_slice.136
  133.2 0.4 broadcast_compare_fusion.4
  133.6 7.0 %fusion.123 = (f32[4,512]{1,0:T(4,128)S(1)}, f32[4,512,1024]{2,1,0:T(8,128)}) fusion(pred[512,1024]{1,0:T(8,128)(4,1)S(1)} %broadcast_compare_fusion.4, bf16[2048,4,64]{0,2,1:T(8,128)(2,1)S(1)} %get-tuple-element.384, s32[]{:T(128)S(6)} %select_n.99, bf16[2048,4,64]{0,2,1:T(8,128)(2,1)} %get-tuple-element.383, s32[]{:T(128)S(6)} %select_n.100), kind=kOutput, calls=%fused_computation.93.clone.1 | convolution fusion | flops 276825088 | bytes 9707528 | tf_op jit(solution)/shard_map/while/body/eval_jaxpr/sub | solution.py:62
  140.6 5.7 %fusion.124 = bf16[4,512,4,64]{1,3,2,0:T(8,128)(2,1)} fusion(bf16[4,512,4,64]{1,3,2,0:T(8,128)(2,1)} %get-tuple-element.364, s32[]{:T(128)} %get-tuple-element.363, f32[4,512,1024]{2,1,0:T(8,128)} %get-tuple-element.336, f32[4,512]{1,0:T(4,128)S(1)} %get-tuple-element.337, bf16[2048,4,64]{0,2,1:T(8,128)(2,1)} %get-tuple-element.381, s32[]{:T(128)S(6)} %select_n.99), kind=kOutput, calls=%fused_computation.12.clone.1 | convolution fusion | flops 272760832 | bytes 9183748 | tf_op jit(solution)/shard_map/while/body/eval_jaxpr/hqk,khd->qhd/dot_general | solution.py:64
  146.4 3.7 %all-to-all-start.1 = ((bf16[4,512,256]{1,2,0:T(8,128)(2,1)}), bf16[4,512,256]{1,2,0:T(8,128)(2,1)S(1)}, u32[]{:S(2)}, u32[]{:S(2)}) async-start(bf16[4,512,256]{1,2,0:T(8,128)(2,1)} %bitcast.17), calls=%async_computation.1 | async-start | bytes 2097152 | tf_op jit(solution)/shard_map/all_to_all | solution.py:109
  150.1 14.2 %all-to-all-done.1 = bf16[4,512,256]{1,2,0:T(8,128)(2,1)S(1)} async-done(((bf16[4,512,256]{1,2,0:T(8,128)(2,1)}), bf16[4,512,256]{1,2,0:T(8,128)(2,1)S(1)}, u32[]{:S(2)}, u32[]{:S(2)}) %all-to-all-start.1) | async-done | bytes 1048608 | tf_op jit(solution)/shard_map/all_to_all | solution.py:109
  164.3 2.9 convert_reduce_fusion
  167.2 0.4 fusion.64
  167.7 0.4 fusion.66
  168.1 2.5 stack.5
  170.6 4.8 %all-to-all-start.2 = ((bf16[4,512,1024]{2,1,0:T(8,128)(2,1)}), bf16[4,512,1024]{2,1,0:T(8,128)(2,1)}, u32[]{:S(2)}, u32[]{:S(2)}) async-start(bf16[4,512,1024]{2,1,0:T(8,128)(2,1)} %stack.5), calls=%async_computation.2 | async-start | bytes 8388608 | tf_op jit(solution)/shard_map/all_to_all | solution.py:13
  175.5 2.3 collective-permute-start.2
  177.8 3.1 collective-permute-start.3
  180.9 53.9 %all-to-all-done.2 = bf16[4,512,1024]{2,1,0:T(8,128)(2,1)} async-done(((bf16[4,512,1024]{2,1,0:T(8,128)(2,1)}), bf16[4,512,1024]{2,1,0:T(8,128)(2,1)}, u32[]{:S(2)}, u32[]{:S(2)}) %all-to-all-start.2) | async-done | bytes 4194336 | tf_op jit(solution)/shard_map/all_to_all | solution.py:13
  234.9 6.1 %convolution_convert_fusion = bf16[2048,768]{0,1:T(8,128)(2,1)S(1)} fusion(bf16[2048,1024]{1,0:T(8,128)(2,1)} %bitcast.22, bf16[2,1024,768]{2,1,0:T(8,128)(2,1)} %param.14), kind=kOutput, calls=%fused_computation.51 | convolution fusion | flops 3222798336 | bytes 8912896 | tf_op jit(solution)/shard_map/dot_general | solution.py:80
  241.1 2.3 collective-permute-start
  243.4 3.1 collective-permute-start.1
  246.9 18.7 %collective-permute-done = bf16[512,512]{0,1:T(8,128)(2,1)S(1)} collective-permute-done((bf16[512,512]{0,1:T(8,128)(2,1)S(1)}, bf16[512,512]{0,1:T(8,128)(2,1)S(1)}, u32[]{:S(2)}, u32[]{:S(2)}) %collective-permute-start) | collective-permute-done | bytes 524320 | tf_op jit(solution)/shard_map/ppermute | solution.py:23
  265.5 2.2 collective-permute-done.1
  268.1 2.0 slice_bitcast_fusion
  270.1 1.1 broadcast.139
  271.2 58.5 %while.25 = (s32[]{:T(128)}, bf16[4,512,4,64]{1,3,2,0:T(8,128)(2,1)}, s32[4]{0:T(128)S(1)}, bf16[3072,4,64]{0,2,1:T(8,128)(2,1)}, s32[2048]{0:T(1024)S(1)}, /*in...) while((s32[]{:T(128)}, ...), condition=%wide.region_11.12_spmd, body=%wide.region_8.11_spmd.sunk | while | flops 550110208 | bytes 19434436 | solution.py:67
  271.2 0.6 dynamic_slice.142
  272.6 0.4 broadcast_compare_fusion.5
  272.9 7.1 %fusion.128 = (f32[4,512]{1,0:T(4,128)S(1)}, f32[4,512,1024]{2,1,0:T(8,128)}) fusion(pred[512,1024]{1,0:T(8,128)(4,1)S(1)} %broadcast_compare_fusion.5, bf16[3072,4,64]{0,2,1:T(8,128)(2,1)} %get-tuple-element.436, s32[]{:T(128)S(6)} %select_n.103, bf16[2048,4,64]{0,2,1:T(8,128)(2,1)S(1)} %get-tuple-element.435, s32[]{:T(128)S(6)} %select_n.104), kind=kOutput, calls=%fused_computation.94.clone.1 | convolution fusion | flops 276825088 | bytes 9707528 | tf_op jit(solution)/shard_map/while/body/eval_jaxpr/sub | solution.py:62
  280.1 5.7 %fusion.129 = bf16[4,512,4,64]{1,3,2,0:T(8,128)(2,1)} fusion(bf16[4,512,4,64]{1,3,2,0:T(8,128)(2,1)} %get-tuple-element.412, s32[]{:T(128)} %get-tuple-element.411, f32[4,512,1024]{2,1,0:T(8,128)} %get-tuple-element.346, f32[4,512]{1,0:T(4,128)S(1)} %get-tuple-element.347, bf16[3072,4,64]{0,2,1:T(8,128)(2,1)} %get-tuple-element.432, s32[]{:T(128)S(6)} %select_n.103), kind=kOutput, calls=%fused_computation.37.clone.1 | convolution fusion | flops 272760832 | bytes 9183748 | tf_op jit(solution)/shard_map/while/body/eval_jaxpr/hqk,khd->qhd/dot_general | solution.py:64
  285.8 0.6 dynamic_slice.142
  287.2 0.4 broadcast_compare_fusion.5
  287.5 7.1 %fusion.128 = (f32[4,512]{1,0:T(4,128)S(1)}, f32[4,512,1024]{2,1,0:T(8,128)}) fusion(pred[512,1024]{1,0:T(8,128)(4,1)S(1)} %broadcast_compare_fusion.5, bf16[3072,4,64]{0,2,1:T(8,128)(2,1)} %get-tuple-element.436, s32[]{:T(128)S(6)} %select_n.103, bf16[2048,4,64]{0,2,1:T(8,128)(2,1)S(1)} %get-tuple-element.435, s32[]{:T(128)S(6)} %select_n.104), kind=kOutput, calls=%fused_computation.94.clone.1 | convolution fusion | flops 276825088 | bytes 9707528 | tf_op jit(solution)/shard_map/while/body/eval_jaxpr/sub | solution.py:62
  294.7 5.7 %fusion.129 = bf16[4,512,4,64]{1,3,2,0:T(8,128)(2,1)} fusion(bf16[4,512,4,64]{1,3,2,0:T(8,128)(2,1)} %get-tuple-element.412, s32[]{:T(128)} %get-tuple-element.411, f32[4,512,1024]{2,1,0:T(8,128)} %get-tuple-element.346, f32[4,512]{1,0:T(4,128)S(1)} %get-tuple-element.347, bf16[3072,4,64]{0,2,1:T(8,128)(2,1)} %get-tuple-element.432, s32[]{:T(128)S(6)} %select_n.103), kind=kOutput, calls=%fused_computation.37.clone.1 | convolution fusion | flops 272760832 | bytes 9183748 | tf_op jit(solution)/shard_map/while/body/eval_jaxpr/hqk,khd->qhd/dot_general | solution.py:64
  300.4 0.6 dynamic_slice.142
  302.2 7.1 %fusion.128 = (f32[4,512]{1,0:T(4,128)S(1)}, f32[4,512,1024]{2,1,0:T(8,128)}) fusion(pred[512,1024]{1,0:T(8,128)(4,1)S(1)} %broadcast_compare_fusion.5, bf16[3072,4,64]{0,2,1:T(8,128)(2,1)} %get-tuple-element.436, s32[]{:T(128)S(6)} %select_n.103, bf16[2048,4,64]{0,2,1:T(8,128)(2,1)S(1)} %get-tuple-element.435, s32[]{:T(128)S(6)} %select_n.104), kind=kOutput, calls=%fused_computation.94.clone.1 | convolution fusion | flops 276825088 | bytes 9707528 | tf_op jit(solution)/shard_map/while/body/eval_jaxpr/sub | solution.py:62
  309.3 5.7 %fusion.129 = bf16[4,512,4,64]{1,3,2,0:T(8,128)(2,1)} fusion(bf16[4,512,4,64]{1,3,2,0:T(8,128)(2,1)} %get-tuple-element.412, s32[]{:T(128)} %get-tuple-element.411, f32[4,512,1024]{2,1,0:T(8,128)} %get-tuple-element.346, f32[4,512]{1,0:T(4,128)S(1)} %get-tuple-element.347, bf16[3072,4,64]{0,2,1:T(8,128)(2,1)} %get-tuple-element.432, s32[]{:T(128)S(6)} %select_n.103), kind=kOutput, calls=%fused_computation.37.clone.1 | convolution fusion | flops 272760832 | bytes 9183748 | tf_op jit(solution)/shard_map/while/body/eval_jaxpr/hqk,khd->qhd/dot_general | solution.py:64
  315.0 0.6 dynamic_slice.142
  316.8 7.1 %fusion.128 = (f32[4,512]{1,0:T(4,128)S(1)}, f32[4,512,1024]{2,1,0:T(8,128)}) fusion(pred[512,1024]{1,0:T(8,128)(4,1)S(1)} %broadcast_compare_fusion.5, bf16[3072,4,64]{0,2,1:T(8,128)(2,1)} %get-tuple-element.436, s32[]{:T(128)S(6)} %select_n.103, bf16[2048,4,64]{0,2,1:T(8,128)(2,1)S(1)} %get-tuple-element.435, s32[]{:T(128)S(6)} %select_n.104), kind=kOutput, calls=%fused_computation.94.clone.1 | convolution fusion | flops 276825088 | bytes 9707528 | tf_op jit(solution)/shard_map/while/body/eval_jaxpr/sub | solution.py:62
  323.9 5.7 %fusion.129 = bf16[4,512,4,64]{1,3,2,0:T(8,128)(2,1)} fusion(bf16[4,512,4,64]{1,3,2,0:T(8,128)(2,1)} %get-tuple-element.412, s32[]{:T(128)} %get-tuple-element.411, f32[4,512,1024]{2,1,0:T(8,128)} %get-tuple-element.346, f32[4,512]{1,0:T(4,128)S(1)} %get-tuple-element.347, bf16[3072,4,64]{0,2,1:T(8,128)(2,1)} %get-tuple-element.432, s32[]{:T(128)S(6)} %select_n.103), kind=kOutput, calls=%fused_computation.37.clone.1 | convolution fusion | flops 272760832 | bytes 9183748 | tf_op jit(solution)/shard_map/while/body/eval_jaxpr/hqk,khd->qhd/dot_general | solution.py:64
  329.6 3.5 all-to-all-start.3
  333.2 14.4 %all-to-all-done.3 = bf16[4,512,256]{1,2,0:T(8,128)(2,1)S(1)} async-done(((bf16[4,512,256]{1,2,0:T(8,128)(2,1)}), bf16[4,512,256]{1,2,0:T(8,128)(2,1)S(1)}, u32[]{:S(2)}, u32[]{:S(2)}) %all-to-all-start.3) | async-done | bytes 1048608 | tf_op jit(solution)/shard_map/all_to_all | solution.py:109
  347.6 3.9 %fusion.71 = bf16[512,1024]{1,0:T(8,128)(2,1)} fusion(bf16[512,1024]{1,0:T(8,128)(2,1)S(1)} %get-tuple-element.247, bf16[512,1024]{0,1:T(8,128)(2,1)S(1)} %bitcast.96, bf16[1,1024,1024]{2,1,0:T(8,128)(2,1)} %all-gather.8.cloned.1.call-done), kind=kOutput, calls=%fused_computation.71 | convolution fusion | flops 1075314688 | bytes 5242880 | tf_op jit(solution)/shard_map/dot_general | solution.py:110
  (52 shorter events, 2.6 us)
Async XLA Ops:
  6.5 1.2 copy-start
  7.8 2.7 copy-start.3
  13.4 5.0 %copy-start.2 = (bf16[2,256,1024]{2,1,0:T(8,128)(2,1)S(1)}, bf16[2,256,1024]{2,1,0:T(8,128)(2,1)}, u32[]{:S(2)}) copy-start(bf16[2,256,1024]{2,1,0:T(8,128)(2,1)} %param.15) | copy-start | bytes 3145732
  13.4 6.1 %copy-start.4 = (s32[512]{0:T(512)S(1)}, s32[512]{0:T(512)}, u32[]{:S(2)}) copy-start(s32[512]{0:T(512)} %param.12) | copy-start | bytes 6148
  13.4 66.0 %all-to-all-start = ((bf16[4,512,1024]{2,1,0:T(8,128)(2,1)}), bf16[4,512,1024]{2,1,0:T(8,128)(2,1)}, u32[]{:S(2)}, u32[]{:S(2)}) async-start(bf16[4,512,1024]{2,1,0:T(8,128)(2,1)} %stack.4), calls=%async_computation | async-start | bytes 8388608 | tf_op jit(solution)/shard_map/all_to_all | solution.py:13
  18.4 131.7 %all-gather.6.cloned.1.call-start = ((), (), s32[]{:S(2)}) async-start(), calls=%async_computation.4 | async-start | bytes 2621440 | tf_op jit(solution)/shard_map/all_gather | solution.py:112
  146.4 17.9 %all-to-all-start.1 = ((bf16[4,512,256]{1,2,0:T(8,128)(2,1)}), bf16[4,512,256]{1,2,0:T(8,128)(2,1)S(1)}, u32[]{:S(2)}, u32[]{:S(2)}) async-start(bf16[4,512,256]{1,2,0:T(8,128)(2,1)} %bitcast.17), calls=%async_computation.1 | async-start | bytes 2097152 | tf_op jit(solution)/shard_map/all_to_all | solution.py:109
  170.6 64.3 %all-to-all-start.2 = ((bf16[4,512,1024]{2,1,0:T(8,128)(2,1)}), bf16[4,512,1024]{2,1,0:T(8,128)(2,1)}, u32[]{:S(2)}, u32[]{:S(2)}) async-start(bf16[4,512,1024]{2,1,0:T(8,128)(2,1)} %stack.5), calls=%async_computation.2 | async-start | bytes 8388608 | tf_op jit(solution)/shard_map/all_to_all | solution.py:13
  175.4 157.8 %all-gather.8.cloned.1.call-start = ((), (), s32[]{:S(2)}) async-start(), calls=%async_computation.5 | async-start | bytes 2621440 | tf_op jit(solution)/shard_map/all_gather | solution.py:112
  175.5 71.0 %collective-permute-start.2 = (bf16[512]{0:T(512)(128)(2,1)S(1)}, bf16[512]{0:T(512)(128)(2,1)S(1)}, u32[]{:S(2)}, u32[]{:S(2)}) collective-permute-start(bf16[512]{0:T(512)(128)(2,1)S(1)} %get-tuple-element.244), channel_id=1, source_target_pairs={{0,4},{4,8},{8,12},{12,16},{16,20},{20,24},{24,28},{28,0},{1,5},{5... | collective-permute-start | bytes 3080 | tf_op jit(solution)/shard_map/ppermute | solution.py:23
  177.8 68.7 %collective-permute-start.3 = (bf16[512]{0:T(512)(128)(2,1)S(1)}, bf16[512]{0:T(512)(128)(2,1)S(1)}, u32[]{:S(2)}, u32[]{:S(2)}) collective-permute-start(bf16[512]{0:T(512)(128)(2,1)S(1)} %get-tuple-element.245), channel_id=1, source_target_pairs={{4,0},{8,4},{12,8},{16,12},{20,16},{24,20},{28,24},{0,28},{5,1},{9... | collective-permute-start | bytes 3080 | tf_op jit(solution)/shard_map/ppermute | solution.py:24
  241.1 24.4 %collective-permute-start = (bf16[512,512]{0,1:T(8,128)(2,1)S(1)}, bf16[512,512]{0,1:T(8,128)(2,1)S(1)}, u32[]{:S(2)}, u32[]{:S(2)}) collective-permute-start(bf16[512,512]{0,1:T(8,128)(2,1)S(1)} %bitcast.100), channel_id=1, source_target_pairs={{0,4},{4,8},{8,12},{12,16},{16,20},{20,24},{24,28},{28,0},{1,5},{5... | collective-permute-start | bytes 1572872 | tf_op jit(solution)/shard_map/ppermute | solution.py:23
  243.4 24.3 %collective-permute-start.1 = (bf16[512,512]{0,1:T(8,128)(2,1)S(1)}, bf16[512,512]{0,1:T(8,128)(2,1)S(1)}, u32[]{:S(2)}, u32[]{:S(2)}) collective-permute-start(bf16[512,512]{0,1:T(8,128)(2,1)S(1)} %bitcast.99), channel_id=1, source_target_pairs={{4,0},{8,4},{12,8},{16,12},{20,16},{24,20},{28,24},{0,28},{5,1},{9... | collective-permute-start | bytes 1572872 | tf_op jit(solution)/shard_map/ppermute | solution.py:24
  329.6 17.9 %all-to-all-start.3 = ((bf16[4,512,256]{1,2,0:T(8,128)(2,1)}), bf16[4,512,256]{1,2,0:T(8,128)(2,1)S(1)}, u32[]{:S(2)}, u32[]{:S(2)}) async-start(bf16[4,512,256]{1,2,0:T(8,128)(2,1)} %bitcast.32), calls=%async_computation.3 | async-start | bytes 2097152 | tf_op jit(solution)/shard_map/all_to_all | solution.py:109
  347.6 3.9 %copy-start.1 = (bf16[512,1024]{1,0:T(8,128)(2,1)S(1)}, bf16[512,1024]{1,0:T(8,128)(2,1)}, u32[]{:S(2)}) copy-start(bf16[512,1024]{1,0:T(8,128)(2,1)} %param.10) | copy-start | bytes 3145732
Sparse Core Ops, SparseCore 0:
  20.8 37.0 all-gather.5
  181.1 33.0 all-gather.7
